TPU v7x, 32 devices: a whole 2x2x4 slice. The times are simulated.
32 devices in a mesh: grp: 4 (over y, core), blk: 8 (over z, x).
Axes of the slice: x: 2, y: 2, z: 4, core: 2. Of those that a mesh axis runs over, the one named last changes fastest.
Arguments:
- primal: float32 [262144], P(('blk', 'grp')), may hold values from -3 to 3
- dual: float32 [131072], P(('blk', 'grp')), may hold values from -3 to 3
- objective: float32 [262144], P(('blk', 'grp')), may hold values from -6 to 6
- lower: float32 [262144], P(('blk', 'grp')), may hold values from -2 to -0.5
- upper: float32 [262144], P(('blk', 'grp')), may hold values from 0.5 to 2
- bound_kind: int32 [262144], P(('blk', 'grp')), may hold values from 0 to 3
- rhs: float32 [131072], P(('blk', 'grp')), may hold values from -6 to 6
- row_kind: int32 [131072], P(('blk', 'grp')), may hold values 0 or 1
- q_tiles: float32 [4, 32, 512, 512], P('grp', 'blk'), may hold values from -0.25 to 0.25
- q_index: int32 [4, 2, 32], P('grp', None, 'blk'), may hold values from 0 to 127
- k_tiles: float32 [4, 48, 512, 512], P('grp', 'blk'), may hold values from -0.25 to 0.25
- k_rows: int32 [4, 48], P('grp', 'blk'), may hold values from 0 to 31
- k_cols: int32 [4, 48], P('grp', 'blk'), may hold values from 0 to 127
Outputs:
- final_primal: float32 [262144], P(('blk', 'grp'))
- final_dual: float32 [131072], P(('blk', 'grp'))
- primal_weight: float32 [], replicated
Inputs may be any that keep to these rules, and one draw needn't show every extreme that they name: `q_index`: row and column tile indices of Hessian tiles, within the column group. `k_rows`: row tile within the tile's dual block. `bound_kind`: 0 free, 1 lower bound only, 2 both bounds, 3 upper bound only.
All inputs are finite; a program needn't handle non-finite values. No bound on the sum of `row_kind` on one device may be relied on, other than what follows from the above.
Results may differ from a plain program's by a relative error of at most 0.00017.
Values sent between devices are 32-bit elements; how exact they have to be, the bound alone decides.
A program may use at most 64 MiB of HBM per device.

v0:
```python
import functools

import jax
import jax.numpy as jnp
from jax import lax
from jax.experimental import pallas as pl
from jax.experimental.pallas import tpu as pltpu
from jax.sharding import PartitionSpec as P

ITERS = 2
EPSILON = 1e-06
STEP_SCALE = 0.5
LANES = 128
CHUNK = 512
MESH = pl.DeviceIdType.MESH
F32 = jnp.float32
BF16 = jnp.bfloat16


def split(values):
    high = values.astype(BF16)
    return high, (values - high.astype(F32)).astype(BF16)


def exchange(axis, count, me, source, target, send, recv):
    def copy(k, slot):
        peer = lax.rem(me + k, count)
        return pltpu.make_async_remote_copy(
            src_ref=source,
            dst_ref=target(me if slot else peer),
            send_sem=send.at[k],
            recv_sem=recv.at[me if slot else peer],
            device_id={axis: peer},
            device_id_type=MESH,
        )

    def start(k, carry):
        copy(k, True).start()
        return carry

    def arrive(k, carry):
        copy(k, False).wait_recv()
        return carry

    def leave(k, carry):
        copy(k, True).wait_send()
        return carry

    lax.fori_loop(1, count, start, 0)
    return (
        lambda: lax.fori_loop(1, count, arrive, 0),
        lambda: lax.fori_loop(1, count, leave, 0),
    )


def segment(ids, start, width, rows, quarters):
    place = lax.broadcasted_iota(jnp.int32, (rows, LANES), 0) * LANES
    place = place + lax.broadcasted_iota(jnp.int32, (rows, LANES), 1) - start
    result = jnp.full((rows, LANES), -1, jnp.int32)
    for p, tile_id in enumerate(ids):
        for q in range(quarters):
            result = jnp.where(place == p * quarters + q, tile_id * quarters + q, result)
    return jnp.where((place >= 0) & (place < width), result, 0)


def kernel(
    n_blk,
    n_grp,
    primal,
    dual,
    objective,
    lower,
    upper,
    bound_kind,
    rhs,
    row_kind,
    q_index,
    k_rows,
    k_cols,
    q_tiles,
    k_tiles,
    x_out,
    y_out,
    w_out,
    raw,
    whi,
    wlo,
    xs,
    ys,
    data,
    rows_data,
    ids_x,
    ids_y,
    sel_x,
    sel_y,
    vals_x,
    vals_y,
    fin,
    cons_now,
    hess_now,
    tile_sem,
    blk_send,
    blk_recv,
    grp_send,
    grp_recv,
):
    blk, grp = lax.axis_index("blk"), lax.axis_index("grp")
    nq, nk = q_tiles.shape[0], k_tiles.shape[0]
    tile = q_tiles.shape[-1]
    quarters = tile // LANES
    own_x, own_y = primal.shape[0], dual.shape[0]
    wide_x, wide_y = vals_x.shape[1] // n_blk, vals_y.shape[1] // n_grp
    prod_x, prod_y = (nq + nk) * quarters, nk * quarters

    loads = []
    for t in range(nk + nq):
        source = k_tiles.at[t] if t < nk else q_tiles.at[t - nk]
        loads.append(pltpu.make_async_copy(source, raw.at[t], tile_sem.at[t]))
        loads[-1].start()

    barrier = pltpu.get_barrier_semaphore()

    def greet(axis, count, me):
        def body(k, carry):
            pl.semaphore_signal(
                barrier, inc=1, device_id={axis: lax.rem(me + k, count)}, device_id_type=MESH
            )
            return carry

        lax.fori_loop(1, count, body, 0)

    greet("blk", n_blk, blk)
    greet("grp", n_grp, grp)

    def slot(ref, index, size):
        return ref.at[pl.ds(pl.multiple_of(index * size, size), size)]

    q_rows = [q_index[0, p] for p in range(nq)]
    q_cols = [q_index[1, p] for p in range(nq)]
    c_rows = [k_rows[0, p] for p in range(nk)]
    c_cols = [k_cols[0, p] for p in range(nk)]
    ids_x[blk] = segment(q_rows + c_cols, blk * wide_x, wide_x, ids_x.shape[1], quarters)
    ids_y[grp] = segment(c_rows, grp * wide_y, wide_y, ids_y.shape[1], quarters)
    kind = bound_kind[...]
    mine_x = pl.ds(pl.multiple_of(blk * own_x, own_x), own_x)
    mine_y = pl.ds(pl.multiple_of(grp * own_y, own_y), own_y)
    data[0, mine_x] = objective[...]
    data[1, mine_x] = jnp.where((kind == 1) | (kind == 2), lower[...], -jnp.inf)
    data[2, mine_x] = jnp.where((kind == 2) | (kind == 3), upper[...], jnp.inf)
    rows_data[0, mine_y] = rhs[...]
    rows_data[1, mine_y] = jnp.where(row_kind[...] == 1, 0.0, -jnp.inf)
    xs[mine_x] = primal[...]
    ys[mine_y] = dual[...]

    pl.semaphore_wait(barrier, n_blk + n_grp - 2)

    leaving = []
    used = {"blk": 0, "grp": 0}

    def share(axis, source, target):
        at = used[axis]
        used[axis] += 1
        count, me = (n_blk, blk) if axis == "blk" else (n_grp, grp)
        send, recv = (blk_send, blk_recv) if axis == "blk" else (grp_send, grp_recv)
        arrive, leave = exchange(
            axis, count, me, source, target, send.at[at], recv.at[at]
        )
        leaving.append(leave)
        return arrive

    y_here = share("grp", dual, lambda s: slot(ys, s, own_y))
    x_here = share("blk", primal, lambda s: slot(xs, s, own_x))
    ids_y_here = share("grp", ids_y.at[grp], lambda s: ids_y.at[s])
    ids_x_here = share("blk", ids_x.at[blk], lambda s: ids_x.at[s])

    def planes(ref, index, size):
        return ref.at[:, pl.ds(pl.multiple_of(index * size, size), size)]

    rows_here = share("grp", planes(rows_data, grp, own_y), lambda s: planes(rows_data, s, own_y))
    data_here = share("blk", planes(data, blk, own_x), lambda s: planes(data, s, own_x))

    for t in range(nk + nq):
        loads[t].wait()
        whi[t], wlo[t] = split(raw[t])

    row = lax.broadcasted_iota(jnp.int32, (16, tile), 0)

    def product(vector, index, t, transposed):
        piece = jnp.concatenate(
            [vector[pl.ds(index * quarters + q, 1), :] for q in range(quarters)], axis=1
        )
        high = piece.astype(BF16).astype(F32)
        left = jnp.where(row == 0, high, jnp.where(row == 1, piece - high, 0.0)).astype(BF16)
        dims = (((1,), (0 if transposed else 1,)), ((), ()))
        out = lax.dot_general(left, whi[t], dims, preferred_element_type=F32)
        out = out + lax.dot_general(left, wlo[t], dims, preferred_element_type=F32)
        return out[0:1] + out[1:2]

    def put(ref, first, values):
        for q in range(quarters):
            ref[pl.ds(first + q, 1), :] = values[:, q * LANES : (q + 1) * LANES]

    def send_gradient(step, scalar):
        mine = vals_x.at[step, pl.ds(pl.multiple_of(blk * wide_x, 8), wide_x)]
        for p in range(nk):
            put(mine, (nq + p) * quarters, -product(ys, c_rows[p], p, True))
        if step == 0:
            x_here()
            hessian()
        mine[: nq * quarters] = hess_now[...]
        mine[prod_x:] = jnp.broadcast_to(scalar, (wide_x - prod_x, LANES))
        return share(
            "blk", mine, lambda s: vals_x.at[step, pl.ds(pl.multiple_of(s * wide_x, 8), wide_x)]
        )

    def hessian():
        for p in range(nq):
            put(hess_now, p * quarters, product(xs, q_cols[p], nk + p, False))

    def constraint(step, scalar):
        mine = vals_y.at[step, pl.ds(pl.multiple_of(grp * wide_y, 8), wide_y)]
        for p in range(nk):
            fresh = product(xs, c_cols[p], p, False)
            for q in range(quarters):
                part = fresh[:, q * LANES : (q + 1) * LANES]
                at = pl.ds(p * quarters + q, 1)
                mine[at, :] = 2.0 * part - cons_now[at, :]
                cons_now[at, :] = part
        mine[prod_y:] = jnp.broadcast_to(scalar, (wide_y - prod_y, LANES))
        return share(
            "grp", mine, lambda s: vals_y.at[step, pl.ds(pl.multiple_of(s * wide_y, 8), wide_y)]
        )

    def gathered(selector, values):
        both = jnp.dot(selector, values, preferred_element_type=F32)
        return both[:, :LANES] + both[:, LANES:]

    def scalar_sum(ref, count, wide, at):
        total = ref[pl.ds(at, 1), :]
        for s in range(1, count):
            total = total + ref[pl.ds(s * wide + at, 1), :]
        return total

    def full_sum(values):
        return jnp.sum(jnp.sum(values, axis=0, keepdims=True), axis=1, keepdims=True)

    chunk_x = min(CHUNK, n_blk * own_x)
    chunk_y = min(CHUNK, n_grp * own_y)

    def selectors():
        ids_y_here()
        ids_x_here()
        for ref, ids, chunk in ((sel_y, ids_y, chunk_y), (sel_x, ids_x, chunk_x)):
            codes = jnp.sum(ids[...], axis=0)

            def body(c, carry):
                base = pl.multiple_of(c * chunk, chunk)
                at = lax.broadcasted_iota(jnp.int32, (chunk, LANES), 0) + base
                for k in range(ref.shape[1] // LANES):
                    hit = at == codes[k : k + 1, :]
                    ref[pl.ds(base, chunk), k * LANES : (k + 1) * LANES] = jnp.where(
                        hit, 1.0, 0.0
                    ).astype(BF16)
                return carry

            lax.fori_loop(0, ref.shape[0] // chunk, body, 0)

    def primal_step(step, tau):
        values = jnp.concatenate(split(vals_x[step]), axis=1)

        def body(c, total):
            at = pl.ds(pl.multiple_of(c * chunk_x, chunk_x), chunk_x)
            gradient = gathered(sel_x[at], values) + data[0, at]
            now = xs[at]
            new = jnp.minimum(jnp.maximum(now - tau * gradient, data[1, at]), data[2, at])
            xs[at] = new
            return total + full_sum((new - now) * (new - now))

        return lax.fori_loop(0, n_blk * own_x // chunk_x, body, jnp.zeros((1, 1), F32))

    def dual_step(step, sigma):
        values = jnp.concatenate(split(vals_y[step]), axis=1)

        def body(c, total):
            at = pl.ds(pl.multiple_of(c * chunk_y, chunk_y), chunk_y)
            extrap = gathered(sel_y[at], values)
            now = ys[at]
            new = jnp.maximum(now + sigma * (rows_data[0, at] - extrap), rows_data[1, at])
            ys[at] = new
            return total + full_sum((new - now) * (new - now))

        return lax.fori_loop(0, n_grp * own_y // chunk_y, body, jnp.zeros((1, 1), F32))

    weight = jnp.ones((1, LANES), F32)
    y_here()
    dual_sq = jnp.zeros((1, 1), F32)
    primal_total = None
    for step in range(ITERS):
        gradient_here = send_gradient(step, dual_sq)
        if step == 0:
            for p in range(nk):
                put(cons_now, p * quarters, product(xs, c_cols[p], p, False))
            selectors()
            data_here()
        gradient_here()
        if step > 0:
            dual_total = scalar_sum(vals_x.at[step], n_blk, wide_x, prod_x)
            weight = jnp.sqrt(
                weight * jnp.sqrt((dual_total + EPSILON) / (primal_total + EPSILON))
            )
        primal_sq = primal_step(step, STEP_SCALE / weight)
        constraint_here = constraint(step, primal_sq)
        if step < ITERS - 1:
            hessian()
        if step == 0:
            rows_here()
        constraint_here()
        primal_total = scalar_sum(vals_y.at[step], n_grp, wide_y, prod_y)
        dual_sq = dual_step(step, STEP_SCALE * weight)

    mine = fin.at[pl.ds(pl.multiple_of(blk * 8, 8), 8)]
    mine[...] = jnp.broadcast_to(dual_sq, (8, LANES))
    last_here = share("blk", mine, lambda s: fin.at[pl.ds(pl.multiple_of(s * 8, 8), 8)])
    x_out[...] = xs[mine_x]
    y_out[...] = ys[mine_y]
    last_here()
    dual_total = scalar_sum(fin, n_blk, 8, 0)
    weight = jnp.sqrt(weight * jnp.sqrt((dual_total + EPSILON) / (primal_total + EPSILON)))
    w_out[...] = weight[:, :1]
    for leave in leaving:
        leave()


def up(value, step):
    return -(-value // step) * step


def shards(
    primal,
    dual,
    objective,
    lower,
    upper,
    bound_kind,
    rhs,
    row_kind,
    q_tiles,
    q_index,
    k_tiles,
    k_rows,
    k_cols,
):
    n_blk, n_grp = lax.axis_size("blk"), lax.axis_size("grp")
    nq, nk, tile = q_tiles.shape[1], k_tiles.shape[1], q_tiles.shape[-1]
    quarters = tile // LANES
    own_x, own_y = primal.shape[0] // LANES, dual.shape[0] // LANES
    wide_x = up((nq + nk) * quarters, 8) + 8
    wide_y = up(nk * quarters, 8) + 8
    depth_x, depth_y = n_blk * wide_x, n_grp * wide_y
    vmem = pl.BlockSpec(memory_space=pltpu.VMEM)
    smem = pl.BlockSpec(memory_space=pltpu.SMEM)
    hbm = pl.BlockSpec(memory_space=pl.ANY)

    def lanes(values):
        return values.reshape(-1, LANES)

    x, y, weight = pl.pallas_call(
        functools.partial(kernel, n_blk, n_grp),
        out_shape=(
            jax.ShapeDtypeStruct((own_x, LANES), F32),
            jax.ShapeDtypeStruct((own_y, LANES), F32),
            jax.ShapeDtypeStruct((1, 1), F32),
        ),
        in_specs=[vmem] * 8 + [smem] * 3 + [hbm] * 2,
        out_specs=(vmem, vmem, vmem),
        scratch_shapes=[
            pltpu.VMEM((nk + nq, tile, tile), F32),
            pltpu.VMEM((nk + nq, tile, tile), BF16),
            pltpu.VMEM((nk + nq, tile, tile), BF16),
            pltpu.VMEM((n_blk * own_x, LANES), F32),
            pltpu.VMEM((n_grp * own_y, LANES), F32),
            pltpu.VMEM((3, n_blk * own_x, LANES), F32),
            pltpu.VMEM((2, n_grp * own_y, LANES), F32),
            pltpu.VMEM((n_blk, up(depth_x // LANES, 8), LANES), jnp.int32),
            pltpu.VMEM((n_grp, up(depth_y // LANES, 8), LANES), jnp.int32),
            pltpu.VMEM((n_blk * own_x, depth_x), BF16),
            pltpu.VMEM((n_grp * own_y, depth_y), BF16),
            pltpu.VMEM((ITERS, depth_x, LANES), F32),
            pltpu.VMEM((ITERS, depth_y, LANES), F32),
            pltpu.VMEM((n_blk * 8, LANES), F32),
            pltpu.VMEM((nk * quarters, LANES), F32),
            pltpu.VMEM((nq * quarters, LANES), F32),
            pltpu.SemaphoreType.DMA((nk + nq,)),
            pltpu.SemaphoreType.DMA((ITERS + 4, n_blk)),
            pltpu.SemaphoreType.DMA((ITERS + 4, n_blk)),
            pltpu.SemaphoreType.DMA((ITERS + 3, n_grp)),
            pltpu.SemaphoreType.DMA((ITERS + 3, n_grp)),
        ],
        compiler_params=pltpu.CompilerParams(
            collective_id=0, has_side_effects=True, vmem_limit_bytes=60 * 1024 * 1024
        ),
    )(
        lanes(primal),
        lanes(dual),
        lanes(objective),
        lanes(lower),
        lanes(upper),
        lanes(bound_kind),
        lanes(rhs),
        lanes(row_kind),
        q_index[0],
        k_rows,
        k_cols,
        q_tiles[0],
        k_tiles[0],
    )
    return x.reshape(-1), y.reshape(-1), weight.reshape(())


def solution(mesh):
    vector = P(("blk", "grp"))
    return jax.shard_map(
        shards,
        mesh=mesh,
        in_specs=(vector,) * 8
        + (
            P("grp", "blk", None, None),
            P("grp", None, "blk"),
            P("grp", "blk", None, None),
            P("grp", "blk"),
            P("grp", "blk"),
        ),
        out_specs=(vector, vector, P()),
        check_vma=False,
    )
```

profile of v0, /device:TPU:0, one launch (start us, length us, event | category | flops | bytes accessed | tf_op | source)
XLA Modules:
  0.0 64.7 jit_solution(11081111355848331165)
XLA Ops:
  0.6 59.7 %shard_map.148 = (f32[64,128]{1,0:T(8,128)}, f32[32,128]{1,0:T(8,128)}, f32[1,1]{1,0:T(1,128)}) custom-call(f32[64,128]{1,0:T(8,128)} %bitcast.16, f32[32,128]{1,0:T(8,128)} %bitcast.22, f32[64,128]{1,0:T(8,128)} %bitcast.17, f32[64,128]{1,0:T(8,128)} %bitcast.18, f32[64,128]{1,0:T(8,128)} %bitcast.19, s32[64,128]{1,0:T(8,128)} %bitcast.20, ...), custom_call_target="tpu_custom_call" | custom-call | tf_op jit(solution)/shard_map/pallas_call | solution.py:367
  60.3 1.4 %copy.19 = f32[8192]{0:T(1024)} copy(f32[8192]{0:T(1024)} %bitcast.21) | data formatting | bytes 65536
  61.7 1.3 %copy.20 = f32[4096]{0:T(1024)} copy(f32[4096]{0:T(1024)} %bitcast.25) | data formatting | bytes 32768
where the time goes:
time: 65.1 us; the launch traced here: 64.7 us
  Pallas kernels  59.7 us (92%)
  local copies, waits for them, and re-layouts  2.7 us (4%)
  between operations  2.38 us (4%)
    pallas_call x1, Pallas kernels, shards(): pl.pallas_call(functools.partial(kernel, n_blk, n_grp), out_shape=(jax.Sh...  59.7 us
    unnamed x2, local copies, waits for them, and re-layouts  2.7 us

commit v1 on v0

--- a/solution.py
+++ b/solution.py
@@ -91,13 +91,15 @@
     rows_data,
     ids_x,
     ids_y,
-    sel_x,
+    sel_h,
+    sel_t,
     sel_y,
-    vals_x,
+    vals_h,
+    vals_t,
     vals_y,
-    fin,
+    sums_x,
+    sums_y,
     cons_now,
-    hess_now,
     tile_sem,
     blk_send,
     blk_recv,
@@ -109,8 +111,9 @@
     tile = q_tiles.shape[-1]
     quarters = tile // LANES
     own_x, own_y = primal.shape[0], dual.shape[0]
-    wide_x, wide_y = vals_x.shape[1] // n_blk, vals_y.shape[1] // n_grp
-    prod_x, prod_y = (nq + nk) * quarters, nk * quarters
+    wide_h, wide_t = nq * quarters, nk * quarters
+    pairs = n_blk // 2
+    code_h = sel_h.shape[1] // LANES
 
     loads = []
     for t in range(nk + nq):
@@ -139,8 +142,10 @@
     q_cols = [q_index[1, p] for p in range(nq)]
     c_rows = [k_rows[0, p] for p in range(nk)]
     c_cols = [k_cols[0, p] for p in range(nk)]
-    ids_x[blk] = segment(q_rows + c_cols, blk * wide_x, wide_x, ids_x.shape[1], quarters)
-    ids_y[grp] = segment(c_rows, grp * wide_y, wide_y, ids_y.shape[1], quarters)
+    code_t = ids_x.shape[1] - code_h
+    ids_x[blk, :code_h] = segment(q_rows, blk * wide_h, wide_h, code_h, quarters)
+    ids_x[blk, code_h:] = segment(c_cols, blk * wide_t, wide_t, code_t, quarters)
+    ids_y[grp] = segment(c_rows, grp * wide_t, wide_t, ids_y.shape[1], quarters)
     kind = bound_kind[...]
     mine_x = pl.ds(pl.multiple_of(blk * own_x, own_x), own_x)
     mine_y = pl.ds(pl.multiple_of(grp * own_y, own_y), own_y)
@@ -170,16 +175,41 @@
 
     y_here = share("grp", dual, lambda s: slot(ys, s, own_y))
     x_here = share("blk", primal, lambda s: slot(xs, s, own_x))
+
     ids_y_here = share("grp", ids_y.at[grp], lambda s: ids_y.at[s])
-    ids_x_here = share("blk", ids_x.at[blk], lambda s: ids_x.at[s])
-
     def planes(ref, index, size):
         return ref.at[:, pl.ds(pl.multiple_of(index * size, size), size)]
 
     rows_here = share("grp", planes(rows_data, grp, own_y), lambda s: planes(rows_data, s, own_y))
-    data_here = share("blk", planes(data, blk, own_x), lambda s: planes(data, s, own_x))
-
-    for t in range(nk + nq):
+    outer, inner = lax.div(blk, 2), lax.rem(blk, 2)
+
+    def passing(at, k, theirs, other):
+        there = lax.rem(outer + k, pairs) * 2
+        if other:
+            sent, got, to = there + inner, there + 1 - inner, outer * 2 + 1 - inner
+        else:
+            sent, got, to = blk, there + inner, there + inner
+        return pltpu.make_async_remote_copy(
+            src_ref=planes(data, sent, own_x),
+            dst_ref=planes(data, got if theirs else sent, own_x),
+            send_sem=blk_send.at[at, k],
+            recv_sem=blk_recv.at[at, got if theirs else sent],
+            device_id={"blk": to},
+            device_id_type=MESH,
+        )
+
+    def each(first, call):
+        def body(k, carry):
+            call(k)
+            return carry
+
+        lax.fori_loop(first, pairs, body, 0)
+
+    def reserve():
+        used["blk"] += 1
+        return used["blk"] - 1
+
+    def unpack(t):
         loads[t].wait()
         whi[t], wlo[t] = split(raw[t])
 
@@ -200,25 +230,28 @@
         for q in range(quarters):
             ref[pl.ds(first + q, 1), :] = values[:, q * LANES : (q + 1) * LANES]
 
-    def send_gradient(step, scalar):
-        mine = vals_x.at[step, pl.ds(pl.multiple_of(blk * wide_x, 8), wide_x)]
+    def row_block(ref, step, index, size):
+        return ref.at[step, pl.ds(pl.multiple_of(index * size, 8), size)]
+
+    def transposed(step):
+        mine = row_block(vals_t, step, blk, wide_t)
         for p in range(nk):
-            put(mine, (nq + p) * quarters, -product(ys, c_rows[p], p, True))
-        if step == 0:
-            x_here()
-            hessian()
-        mine[: nq * quarters] = hess_now[...]
-        mine[prod_x:] = jnp.broadcast_to(scalar, (wide_x - prod_x, LANES))
-        return share(
-            "blk", mine, lambda s: vals_x.at[step, pl.ds(pl.multiple_of(s * wide_x, 8), wide_x)]
-        )
-
-    def hessian():
+            put(mine, p * quarters, -product(ys, c_rows[p], p, True))
+        return share("blk", mine, lambda s: row_block(vals_t, step, s, wide_t))
+
+    def hessian(step):
+        mine = row_block(vals_h, step, blk, wide_h)
         for p in range(nq):
-            put(hess_now, p * quarters, product(xs, q_cols[p], nk + p, False))
-
-    def constraint(step, scalar):
-        mine = vals_y.at[step, pl.ds(pl.multiple_of(grp * wide_y, 8), wide_y)]
+            put(mine, p * quarters, product(xs, q_cols[p], nk + p, False))
+        return share("blk", mine, lambda s: row_block(vals_h, step, s, wide_h))
+
+    def spread(axis, ref, step, value):
+        me = blk if axis == "blk" else grp
+        ref[step, me] = jnp.broadcast_to(value, (1, LANES))
+        return share(axis, ref.at[step, me], lambda s: ref.at[step, s])
+
+    def constraint(step):
+        mine = row_block(vals_y, step, grp, wide_t)
         for p in range(nk):
             fresh = product(xs, c_cols[p], p, False)
             for q in range(quarters):
@@ -226,19 +259,21 @@
                 at = pl.ds(p * quarters + q, 1)
                 mine[at, :] = 2.0 * part - cons_now[at, :]
                 cons_now[at, :] = part
-        mine[prod_y:] = jnp.broadcast_to(scalar, (wide_y - prod_y, LANES))
-        return share(
-            "grp", mine, lambda s: vals_y.at[step, pl.ds(pl.multiple_of(s * wide_y, 8), wide_y)]
+        return share("grp", mine, lambda s: row_block(vals_y, step, s, wide_t))
+
+    def parts(values):
+        return jnp.concatenate(split(values), axis=1)
+
+    def gathered(*terms):
+        both = sum(
+            jnp.dot(selector, values, preferred_element_type=F32) for selector, values in terms
         )
-
-    def gathered(selector, values):
-        both = jnp.dot(selector, values, preferred_element_type=F32)
         return both[:, :LANES] + both[:, LANES:]
 
-    def scalar_sum(ref, count, wide, at):
-        total = ref[pl.ds(at, 1), :]
+    def scalar_sum(ref, step, count):
+        total = ref[step, 0]
         for s in range(1, count):
-            total = total + ref[pl.ds(s * wide + at, 1), :]
+            total = total + ref[step, s]
         return total
 
     def full_sum(values):
@@ -250,8 +285,12 @@
     def selectors():
         ids_y_here()
         ids_x_here()
-        for ref, ids, chunk in ((sel_y, ids_y, chunk_y), (sel_x, ids_x, chunk_x)):
-            codes = jnp.sum(ids[...], axis=0)
+        codes_x, codes_y = jnp.sum(ids_x[...], axis=0), jnp.sum(ids_y[...], axis=0)
+        for ref, codes, chunk in (
+            (sel_h, codes_x[:code_h], chunk_x),
+            (sel_t, codes_x[code_h:], chunk_x),
+            (sel_y, codes_y, chunk_y),
+        ):
 
             def body(c, carry):
                 base = pl.multiple_of(c * chunk, chunk)
@@ -266,11 +305,14 @@
             lax.fori_loop(0, ref.shape[0] // chunk, body, 0)
 
     def primal_step(step, tau):
-        values = jnp.concatenate(split(vals_x[step]), axis=1)
+        from_h, from_t = parts(vals_h[step]), parts(vals_t[step])
 
         def body(c, total):
             at = pl.ds(pl.multiple_of(c * chunk_x, chunk_x), chunk_x)
-            gradient = gathered(sel_x[at], values) + data[0, at]
+            gradient = gathered(
+                (sel_h[at, : n_blk * wide_h], from_h), (sel_t[at, : n_blk * wide_t], from_t)
+            )
+            gradient = gradient + data[0, at]
             now = xs[at]
             new = jnp.minimum(jnp.maximum(now - tau * gradient, data[1, at]), data[2, at])
             xs[at] = new
@@ -279,11 +321,11 @@
         return lax.fori_loop(0, n_blk * own_x // chunk_x, body, jnp.zeros((1, 1), F32))
 
     def dual_step(step, sigma):
-        values = jnp.concatenate(split(vals_y[step]), axis=1)
+        values = parts(vals_y[step])
 
         def body(c, total):
             at = pl.ds(pl.multiple_of(c * chunk_y, chunk_y), chunk_y)
-            extrap = gathered(sel_y[at], values)
+            extrap = gathered((sel_y[at, : n_grp * wide_t], values))
             now = ys[at]
             new = jnp.maximum(now + sigma * (rows_data[0, at] - extrap), rows_data[1, at])
             ys[at] = new
@@ -292,41 +334,60 @@
         return lax.fori_loop(0, n_grp * own_y // chunk_y, body, jnp.zeros((1, 1), F32))
 
     weight = jnp.ones((1, LANES), F32)
+    for t in range(nk):
+        unpack(t)
     y_here()
-    dual_sq = jnp.zeros((1, 1), F32)
-    primal_total = None
+    transposed_here = transposed(0)
+    ids_x_here = share("blk", ids_x.at[blk], lambda s: ids_x.at[s])
+    at_own, at_other = reserve(), reserve()
+    passing(at_other, 0, False, True).start()
+    each(1, lambda k: passing(at_own, k, False, False).start())
+    for t in range(nk, nk + nq):
+        unpack(t)
+    x_here()
+    hessian_here = hessian(0)
+    for p in range(nk):
+        put(cons_now, p * quarters, product(xs, c_cols[p], p, False))
+
+    def forward(k):
+        passing(at_own, k, True, False).wait_recv()
+        passing(at_other, k, False, True).start()
+
+    each(1, forward)
+    selectors()
+    each(0, lambda k: passing(at_other, k, True, True).wait_recv())
     for step in range(ITERS):
-        gradient_here = send_gradient(step, dual_sq)
-        if step == 0:
-            for p in range(nk):
-                put(cons_now, p * quarters, product(xs, c_cols[p], p, False))
-            selectors()
-            data_here()
-        gradient_here()
+        hessian_here()
+        transposed_here()
         if step > 0:
-            dual_total = scalar_sum(vals_x.at[step], n_blk, wide_x, prod_x)
+            dual_here()
+            dual_total = scalar_sum(sums_x, step - 1, n_blk)
             weight = jnp.sqrt(
                 weight * jnp.sqrt((dual_total + EPSILON) / (primal_total + EPSILON))
             )
         primal_sq = primal_step(step, STEP_SCALE / weight)
-        constraint_here = constraint(step, primal_sq)
+        constraint_here = constraint(step)
+        primal_here = spread("grp", sums_y, step, primal_sq)
         if step < ITERS - 1:
-            hessian()
+            hessian_here = hessian(step + 1)
         if step == 0:
             rows_here()
         constraint_here()
-        primal_total = scalar_sum(vals_y.at[step], n_grp, wide_y, prod_y)
         dual_sq = dual_step(step, STEP_SCALE * weight)
-
-    mine = fin.at[pl.ds(pl.multiple_of(blk * 8, 8), 8)]
-    mine[...] = jnp.broadcast_to(dual_sq, (8, LANES))
-    last_here = share("blk", mine, lambda s: fin.at[pl.ds(pl.multiple_of(s * 8, 8), 8)])
+        dual_here = spread("blk", sums_x, step, dual_sq)
+        if step < ITERS - 1:
+            transposed_here = transposed(step + 1)
+        primal_here()
+        primal_total = scalar_sum(sums_y, step, n_grp)
+
     x_out[...] = xs[mine_x]
     y_out[...] = ys[mine_y]
-    last_here()
-    dual_total = scalar_sum(fin, n_blk, 8, 0)
+    dual_here()
+    dual_total = scalar_sum(sums_x, ITERS - 1, n_blk)
     weight = jnp.sqrt(weight * jnp.sqrt((dual_total + EPSILON) / (primal_total + EPSILON)))
     w_out[...] = weight[:, :1]
+    each(0, lambda k: passing(at_other, k, False, True).wait_send())
+    each(1, lambda k: passing(at_own, k, False, False).wait_send())
     for leave in leaving:
         leave()
 
@@ -354,9 +415,9 @@
     nq, nk, tile = q_tiles.shape[1], k_tiles.shape[1], q_tiles.shape[-1]
     quarters = tile // LANES
     own_x, own_y = primal.shape[0] // LANES, dual.shape[0] // LANES
-    wide_x = up((nq + nk) * quarters, 8) + 8
-    wide_y = up(nk * quarters, 8) + 8
-    depth_x, depth_y = n_blk * wide_x, n_grp * wide_y
+    wide_h, wide_t = nq * quarters, nk * quarters
+    code_h, code_t = up(n_blk * wide_h, LANES), up(n_blk * wide_t, LANES)
+    code_y = up(n_grp * wide_t, LANES)
     vmem = pl.BlockSpec(memory_space=pltpu.VMEM)
     smem = pl.BlockSpec(memory_space=pltpu.SMEM)
     hbm = pl.BlockSpec(memory_space=pl.ANY)
@@ -381,20 +442,22 @@
             pltpu.VMEM((n_grp * own_y, LANES), F32),
             pltpu.VMEM((3, n_blk * own_x, LANES), F32),
             pltpu.VMEM((2, n_grp * own_y, LANES), F32),
-            pltpu.VMEM((n_blk, up(depth_x // LANES, 8), LANES), jnp.int32),
-            pltpu.VMEM((n_grp, up(depth_y // LANES, 8), LANES), jnp.int32),
-            pltpu.VMEM((n_blk * own_x, depth_x), BF16),
-            pltpu.VMEM((n_grp * own_y, depth_y), BF16),
-            pltpu.VMEM((ITERS, depth_x, LANES), F32),
-            pltpu.VMEM((ITERS, depth_y, LANES), F32),
-            pltpu.VMEM((n_blk * 8, LANES), F32),
+            pltpu.VMEM((n_blk, (code_h + code_t) // LANES, LANES), jnp.int32),
+            pltpu.VMEM((n_grp, code_y // LANES, LANES), jnp.int32),
+            pltpu.VMEM((n_blk * own_x, code_h), BF16),
+            pltpu.VMEM((n_blk * own_x, code_t), BF16),
+            pltpu.VMEM((n_grp * own_y, code_y), BF16),
+            pltpu.VMEM((ITERS, n_blk * wide_h, LANES), F32),
+            pltpu.VMEM((ITERS, n_blk * wide_t, LANES), F32),
+            pltpu.VMEM((ITERS, n_grp * wide_t, LANES), F32),
+            pltpu.VMEM((ITERS, n_blk, 1, LANES), F32),
+            pltpu.VMEM((ITERS, n_grp, 1, LANES), F32),
             pltpu.VMEM((nk * quarters, LANES), F32),
-            pltpu.VMEM((nq * quarters, LANES), F32),
             pltpu.SemaphoreType.DMA((nk + nq,)),
-            pltpu.SemaphoreType.DMA((ITERS + 4, n_blk)),
-            pltpu.SemaphoreType.DMA((ITERS + 4, n_blk)),
-            pltpu.SemaphoreType.DMA((ITERS + 3, n_grp)),
-            pltpu.SemaphoreType.DMA((ITERS + 3, n_grp)),
+            pltpu.SemaphoreType.DMA((3 * ITERS + 4, n_blk)),
+            pltpu.SemaphoreType.DMA((3 * ITERS + 4, n_blk)),
+            pltpu.SemaphoreType.DMA((2 * ITERS + 3, n_grp)),
+            pltpu.SemaphoreType.DMA((2 * ITERS + 3, n_grp)),
         ],
         compiler_params=pltpu.CompilerParams(
             collective_id=0, has_side_effects=True, vmem_limit_bytes=60 * 1024 * 1024

time: 65.1 us -> 60.2 us (0.925)
  Pallas kernels: 59.7 us -> 54.8 us
    pallas_call x1, Pallas kernels: 59.7 us -> 54.8 us  [shards(): pl.pallas_call(functools.partial(kernel, n_blk, n_grp), out_shape=(jax.Sh...]
where the time goes in v1:
time: 60.2 us; the launch traced here: 59.9 us
  Pallas kernels  54.8 us (91%)
  local copies, waits for them, and re-layouts  2.7 us (4%)
  between operations  2.38 us (4%)
    pallas_call x1, Pallas kernels, shards(): pl.pallas_call(functools.partial(kernel, n_blk, n_grp), out_shape=(jax.Sh...  54.8 us
    unnamed x2, local copies, waits for them, and re-layouts  2.7 us

profile of v1, /device:TPU:0, one launch (start us, length us, event | category | flops | bytes accessed | tf_op | source)
XLA Modules:
  0.0 59.9 jit_solution(5208910010367946398)
XLA Ops:
  0.6 54.8 %shard_map.148 = (f32[64,128]{1,0:T(8,128)}, f32[32,128]{1,0:T(8,128)}, f32[1,1]{1,0:T(1,128)}) custom-call(f32[64,128]{1,0:T(8,128)} %bitcast.16, f32[32,128]{1,0:T(8,128)} %bitcast.22, f32[64,128]{1,0:T(8,128)} %bitcast.17, f32[64,128]{1,0:T(8,128)} %bitcast.18, f32[64,128]{1,0:T(8,128)} %bitcast.19, s32[64,128]{1,0:T(8,128)} %bitcast.20, ...), custom_call_target="tpu_custom_call" | custom-call | tf_op jit(solution)/shard_map/pallas_call | solution.py:428
  55.5 1.4 %copy.19 = f32[8192]{0:T(1024)} copy(f32[8192]{0:T(1024)} %bitcast.21) | data formatting | bytes 65536
  56.9 1.3 %copy.20 = f32[4096]{0:T(1024)} copy(f32[4096]{0:T(1024)} %bitcast.25) | data formatting | bytes 32768
